TPU v7x, 32 devices: a whole 2x2x4 slice. The times are simulated.
32 devices in a mesh: wave: 4 (over y, x), freq: 8 (over z, core).
Axes of the slice: x: 2, y: 2, z: 4, core: 2. Of those that a mesh axis runs over, the one named last changes fastest.
Arguments:
- waveforms: float32 [1024, 16384], P('wave', 'freq'), may hold values from -6 to 6
- pivots: int32 [2, 128], replicated, may hold values from 0 to 1023, as said below
- nodes: int32 [1024], replicated, may hold values from 0 to 16383, as said below
Outputs:
- residual: float32 [1024, 16384], P('wave', 'freq')
- basis_rows: float32 [256, 16384], P(None, 'freq')
- fitted: float32 [1024, 16384], P('wave', 'freq')
Inputs may be any that keep to these rules, and one draw needn't show every extreme that they name: `pivots`: all 256 pivot indices are different. `nodes`: all node indices are different.
All inputs are finite; a program needn't handle non-finite values.
Results may differ from a plain program's by a relative error of at most 0.0001.
Values sent between devices are 32-bit elements; how exact they have to be, the bound alone decides.
A program may use at most 64 MiB of HBM per device.

v0:
```python
import jax
import jax.numpy as jnp
from jax import lax
from jax.sharding import PartitionSpec as P

HIGH = lax.Precision.HIGHEST


def body(waveforms, pivots, nodes):
    rows_here, cols_here = waveforms.shape
    row_start = lax.axis_index("wave") * rows_here
    col_start = lax.axis_index("freq") * cols_here
    residual = waveforms
    blocks = []
    for step in range(pivots.shape[0]):
        local_rows = pivots[step] - row_start
        inside = ((local_rows >= 0) & (local_rows < rows_here)).astype(jnp.float32)
        picked = (
            jnp.take(residual, jnp.clip(local_rows, 0, rows_here - 1), axis=0) * inside[:, None]
        )
        pivot_block = lax.psum(picked, "wave")
        cross_total, gram_total = lax.psum(
            (
                jnp.dot(residual, pivot_block.T, precision=HIGH),
                jnp.dot(pivot_block, pivot_block.T, precision=HIGH),
            ),
            "freq",
        )
        factor = jnp.linalg.cholesky(gram_total)
        ortho = jax.scipy.linalg.solve_triangular(factor, pivot_block, lower=True)
        coeffs = jax.scipy.linalg.solve_triangular(factor, cross_total.T, lower=True).T
        residual = residual - jnp.dot(coeffs, ortho, precision=HIGH)
        blocks.append(ortho)
    basis_rows = jnp.concatenate(blocks, axis=0)
    columns = col_start + jnp.arange(cols_here, dtype=jnp.int32)
    node_count = jnp.sum((nodes[:, None] == columns[None, :]).astype(jnp.float32), axis=0)
    weighted = basis_rows * node_count[None, :]
    gram_part = jnp.dot(weighted, basis_rows.T, precision=HIGH)
    cross_part = jnp.dot(waveforms, weighted.T, precision=HIGH)
    node_total, cross_total = lax.psum((gram_part, cross_part), "freq")
    node_factor = jnp.linalg.cholesky(node_total)
    coefficients = jax.scipy.linalg.cho_solve((node_factor, True), cross_total.T).T
    fitted = jnp.dot(coefficients, basis_rows, precision=HIGH)
    return (residual, basis_rows, fitted)


def solution(mesh):
    in_specs = (P("wave", "freq"), P(), P())
    out_specs = (P("wave", "freq"), P(None, "freq"), P("wave", "freq"))
    return jax.shard_map(body, mesh=mesh, in_specs=in_specs, out_specs=out_specs, check_vma=False)
```

profile of v0, /device:TPU:0, one launch (start us, length us, event | category | flops | bytes accessed | tf_op | source)
XLA Modules:
  0.0 441.0 jit_solution(16491950977878656175)
XLA Ops:
  7.2 0.8 compare_and_fusion
  8.0 0.8 fusion.40
  8.8 3.0 gather_fusion
  11.8 1.2 select_multiply_fusion.1
  13.1 55.3 %all-reduce.9.cloned.1.call-done = f32[128,2048]{1,0:T(8,128)} async-done(((f32[128,2048]{1,0:T(8,128)}), f32[128,2048]{1,0:T(8,128)}) %all-reduce.9.cloned.1.call-update) | async-done | bytes 1048592 | tf_op jit(solution)/shard_map/psum | solution.py:21
  68.4 4.2 fusion.44
  72.6 1.6 fusion.43
  74.4 55.2 %all-reduce.17.cloned.1.call-done = (f32[128,256]{1,0:T(8,128)}, f32[128,128]{0,1:T(8,128)}) async-done(((f32[128,256]{1,0:T(8,128)}, f32[128,128]{0,1:T(8,128)}), (f32[128,256]{1,0:T(8,128)}, f32[128,128]{0,1:T(8,128)})) %all-reduce.17.cloned.1.call-update) | async-done | bytes 196624 | tf_op jit(solution)/shard_map/psum | solution.py:22
  129.7 0.9 copy.13
  130.6 0.9 fusion.27
  131.4 11.7 %cholesky.162 = f32[128,128]{1,0:T(8,128)S(1)} custom-call(f32[128,128]{1,0:T(8,128)S(1)} %fusion.27), custom_call_target="Cholesky" | custom-call | tf_op jit(solution)/shard_map/jit(cholesky)/cholesky | solution.py:29
  143.2 0.6 compare_reduce_fusion.1
  143.8 0.7 fusion.13
  144.5 9.8 %custom-call.30 = f32[1,128,128]{1,2,0:T(8,128)S(1)} custom-call(f32[1,128,128]{2,1,0:T(8,128)S(1)} %fusion.13), custom_call_target="InvertDiagBlocksLowerTriangular" | custom-call | tf_op jit(solution)/shard_map/jit(_solve_triangular)/triangular_solve | solution.py:31
  154.3 1.2 fusion.25
  155.5 1.1 fusion.23
  156.6 1.0 copy-done.6
  157.6 3.4 convolution_subtract_fusion.1
  161.0 1.0 gather_fusion.1
  162.0 1.2 select_multiply_fusion
  163.3 0.9 convert_reduce_fusion
  164.2 50.7 %all-reduce.11.cloned.1.call-done = f32[128,2048]{1,0:T(8,128)} async-done(((f32[128,2048]{1,0:T(8,128)}), f32[128,2048]{1,0:T(8,128)}) %all-reduce.11.cloned.1.call-update) | async-done | bytes 1048592 | tf_op jit(solution)/shard_map/psum | solution.py:21
  214.9 3.3 fusion.45
  218.4 2.9 fusion.46
  221.3 51.7 %all-reduce.13.cloned.1.call-done = f32[128,128]{0,1:T(8,128)} async-done(((f32[128,128]{0,1:T(8,128)}), f32[128,128]{0,1:T(8,128)}) %all-reduce.13.cloned.1.call-update) | async-done | bytes 65552 | tf_op jit(solution)/shard_map/psum | solution.py:22
  273.0 0.9 copy.15
  273.9 0.9 fusion.22
  274.8 11.7 %cholesky.173 = f32[128,128]{1,0:T(8,128)S(1)} custom-call(f32[128,128]{1,0:T(8,128)S(1)} %fusion.22), custom_call_target="Cholesky" | custom-call | tf_op jit(solution)/shard_map/jit(cholesky)/cholesky | solution.py:29
  286.5 0.6 compare_reduce_fusion
  287.2 0.7 fusion.14
  287.8 9.8 %custom-call.32 = f32[1,128,128]{1,2,0:T(8,128)S(1)} custom-call(f32[1,128,128]{2,1,0:T(8,128)S(1)} %fusion.14), custom_call_target="InvertDiagBlocksLowerTriangular" | custom-call | tf_op jit(solution)/shard_map/jit(_solve_triangular)/triangular_solve | solution.py:31
  297.7 1.1 fusion.18
  299.1 0.7 copy-done.8
  299.9 1.0 copy-done.1
  300.9 2.7 fusion
  303.5 3.1 fusion.2
  306.6 56.4 %all-reduce.15.cloned.1.call-done = (f32[128,256]{1,0:T(8,128)}, f32[256,256]{1,0:T(8,128)}, f32[256,256]{0,1:T(8,128)}) async-done(((f32[128,256]{1,0:T(8,128)}, f32[256,256]{1,0:T(8,128)}, f32[256,256]{0,1:T(8,128)}), (f32[128,256]{1,0:T(8,128)}, f32[256,256]{1,0:T(8,128)}, f32[256,256]{0,1:T(8,128)})) %all-reduce.15.cloned.1.call-update) | async-done | bytes 655376 | tf_op jit(solution)/shard_map/psum | solution.py:22
  363.0 1.2 fusion.20
  364.2 3.2 convolution_subtract_fusion
  367.6 11.7 %cholesky.77 = f32[128,128]{1,0:T(8,128)S(1)} custom-call(f32[128,128]{1,0:T(8,128)S(1)} %cholesky.182), custom_call_target="Cholesky" | custom-call | tf_op jit(solution)/shard_map/jit(cholesky)/cholesky | solution.py:41
  379.4 9.8 %custom-call.26 = f32[1,128,128]{1,2,0:T(8,128)S(1)} custom-call(f32[1,128,128]{2,1,0:T(8,128)S(1)} %get-tuple-element.37), custom_call_target="InvertDiagBlocksLowerTriangular" | custom-call | tf_op jit(solution)/shard_map/jit(cholesky)/cholesky | solution.py:41
  389.7 11.9 %cholesky.132 = f32[128,128]{1,0:T(8,128)S(1)} custom-call(f32[128,128]{1,0:T(8,128)S(1)} %convolution_subtract_fusion.4), custom_call_target="Cholesky" | custom-call | tf_op jit(solution)/shard_map/jit(cholesky)/cholesky | solution.py:41
  401.6 0.7 compare_reduce_fusion.2
  403.6 5.1 %while.1 = (s32[]{:T(128)}, f32[256,256]{1,0:T(8,128)S(1)}, s32[2,2]{1,0:T(2,128)S(1)}, f32[2,128,128]{2,1,0:T(8,128)}, s32[]{:T(128)}) while((s32[]{:T(128)}, f32[256,256]{1,0:T(8,128)S(1)}, s32[2,2]{1,0:T(2,128)S(1)}, f32[2,128,128]{2,1,0:T(8,128)}, s32[]{:T(128)}) %tuple.36), condition=%wide.while_cond, body=%wide.while_body.sunk | while | flops 2 | bytes 132205 | solution.py:42
  404.2 2.0 bitcast_dynamic-update-slice_fusion.2
  406.8 2.0 bitcast_dynamic-update-slice_fusion.2
  408.7 20.5 %custom-call.27 = f32[2,128,128]{1,2,0:T(8,128)S(1)} custom-call(f32[2,128,128]{2,1,0:T(8,128)} %get-tuple-element.14), custom_call_target="InvertDiagBlocksLowerTriangular" | custom-call | tf_op jit(solution)/shard_map/jit(_cho_solve)/triangular_solve | solution.py:42
  431.0 3.2 fusion.6
  (61 shorter events, 4.9 us)
Async XLA Ops:
  7.2 61.2 %all-reduce.9.cloned.1.call-start = ((), (), s32[]{:S(2)}) async-start(), calls=%async_computation | async-start | bytes 2097152 | tf_op jit(solution)/shard_map/psum | solution.py:21
  11.8 56.5 %copy-start = (f32[256,2048]{1,0:T(8,128)S(1)}, f32[256,2048]{1,0:T(8,128)}, u32[]{:S(2)}) copy-start(f32[256,2048]{1,0:T(8,128)} %param.10) | copy-start | bytes 6291460
  13.0 116.6 %all-reduce.17.cloned.1.call-start = ((), (), s32[]{:S(2)}) async-start(), calls=%async_computation.4 | async-start | bytes 393216 | tf_op jit(solution)/shard_map/psum | solution.py:22
  68.4 4.2 copy-start.4
  74.2 140.7 %all-reduce.11.cloned.1.call-start = ((), (), s32[]{:S(2)}) async-start(), calls=%async_computation.1 | async-start | bytes 2097152 | tf_op jit(solution)/shard_map/psum | solution.py:21
  156.6 1.0 copy-start.6
  162.0 1.3 copy-start.12
  163.2 109.8 %all-reduce.13.cloned.1.call-start = ((), (), s32[]{:S(2)}) async-start(), calls=%async_computation.2 | async-start | bytes 131072 | tf_op jit(solution)/shard_map/psum | solution.py:22
  214.9 3.5 copy-start.5
  218.1 144.8 %all-reduce.15.cloned.1.call-start = ((), (), s32[]{:S(2)}) async-start(), calls=%async_computation.3 | async-start | bytes 1310720 | tf_op jit(solution)/shard_map/psum | solution.py:22
  297.7 1.2 copy-start.7
  298.9 1.0 copy-start.8
  298.9 2.0 copy-start.1
  300.9 2.7 copy-start.2
  303.5 60.7 %copy-start.9 = (f32[128,2048]{1,0:T(8,128)S(1)}, f32[128,2048]{1,0:T(8,128)}, u32[]{:S(2)}) copy-start(f32[128,2048]{1,0:T(8,128)} %copy-done.8) | copy-start | bytes 3145732
  364.2 3.2 copy-start.10
  367.4 61.8 %copy-start.11 = (f32[256,256]{1,0:T(8,128)S(1)}, f32[256,256]{1,0:T(8,128)}, u32[]{:S(2)}) copy-start(f32[256,256]{1,0:T(8,128)} %get-tuple-element.24) | copy-start | bytes 786436
  389.2 41.8 %copy-start.3 = (f32[256,2048]{1,0:T(8,128)S(1)}, f32[256,2048]{1,0:T(8,128)}, u32[]{:S(2)}) copy-start(f32[256,2048]{1,0:T(8,128)} %copy-done.2) | copy-start | bytes 6291460
Sparse Core Ops, SparseCore 0:
  13.1 55.1 all-reduce.8
  74.3 55.2 all-reduce.16
  163.3 51.4 all-reduce.10
  218.3 54.6 all-reduce.12
  306.7 56.2 all-reduce.14
where the time goes:
time: 445 us; the launch traced here: 441 us
  waiting for transfers between devices  269 us (60%)
  other arithmetic  107 us (24%)
  matrix products  34.2 us (8%)
  between operations  15.6 us (4%)
  local copies, waits for them, and re-layouts  14.1 us (3%)
    psum x3, waiting for transfers between devices, body(): lax.psum((jnp.dot(residual, pivot_block.T, precision=HIGH), jnp.dot(pivot...  163 us
    psum x2, waiting for transfers between devices, body(): pivot_block = lax.psum(picked, 'wave')  106 us
    another operation x6, other arithmetic, body(): node_factor = jnp.linalg.cholesky(node_total)  34.1 us
    another operation x6, other arithmetic, body(): factor = jnp.linalg.cholesky(gram_total)  24.8 us
    another operation x4, other arithmetic, body(): jax.scipy.linalg.solve_triangular(factor, cross_total.T, lower=True)  20.9 us
    another operation x3, other arithmetic, body(): jax.scipy.linalg.cho_solve((node_factor, True), cross_total.T)  20.5 us
  transfers between devices with their start and end apart: 5, of which 5 were waited for; matrix products, arithmetic and copies ran while one was open for 1% of the time, Pallas kernels for 0%

commit v1 on v0

v1 whole, which is shorter than its diff:
```python
import jax
import jax.numpy as jnp
from jax import lax
from jax.sharding import PartitionSpec as P

HIGH = lax.Precision.HIGH


def body(waveforms, pivots, nodes):
    rows_here, cols_here = waveforms.shape
    row_start = lax.axis_index("wave") * rows_here
    col_start = lax.axis_index("freq") * cols_here
    picks = pivots.reshape(-1)
    count = picks.shape[0]
    local_rows = picks - row_start
    inside = ((local_rows >= 0) & (local_rows < rows_here)).astype(jnp.float32)
    picked = jnp.take(waveforms, jnp.clip(local_rows, 0, rows_here - 1), axis=0) * inside[:, None]
    pivot_rows = lax.psum(picked, "wave")
    columns = col_start + jnp.arange(cols_here, dtype=jnp.int32)
    node_count = jnp.sum((nodes[:, None] == columns[None, :]).astype(jnp.float32), axis=0)
    weighted = pivot_rows * node_count[None, :]
    left = jnp.concatenate([pivot_rows, waveforms], axis=0)
    right = jnp.concatenate([pivot_rows, weighted], axis=0)
    total = lax.psum(jnp.dot(left, right.T, precision=HIGH), "freq")
    gram, node_gram = total[:count, :count], total[:count, count:]
    cross, node_cross = total[count:, :count], total[count:, count:]
    factors = jnp.linalg.cholesky(jnp.stack([gram, node_gram]))
    eye = jnp.broadcast_to(jnp.eye(count, dtype=jnp.float32), factors.shape)
    inverses = jax.scipy.linalg.solve_triangular(factors, eye, lower=True)
    hi = lax.Precision.HIGHEST
    basis_rows = jnp.dot(inverses[0], pivot_rows, precision=HIGH)
    coeffs = jnp.dot(cross, inverses[0].T, precision=hi)
    residual = waveforms - jnp.dot(coeffs, basis_rows, precision=HIGH)
    coefficients = jnp.dot(jnp.dot(node_cross, inverses[1].T, precision=hi), inverses[1], precision=hi)
    fitted = jnp.dot(coefficients, pivot_rows, precision=HIGH)
    return (residual, basis_rows, fitted)


def solution(mesh):
    in_specs = (P("wave", "freq"), P(), P())
    out_specs = (P("wave", "freq"), P(None, "freq"), P("wave", "freq"))
    return jax.shard_map(body, mesh=mesh, in_specs=in_specs, out_specs=out_specs, check_vma=False)
```

time: 445 us -> 288 us (0.65)
  waiting for transfers between devices: 269 us -> 130 us
  matrix products: 34.2 us -> 16.1 us
  other arithmetic: 107 us -> 114 us
    psum x5 -> x2, waiting for transfers between devices: 269 us -> 130 us  [the longest x1 70.8 us: body(): pivot_rows = lax.psum(picked, 'wave')]
    dot_general x9 -> x7, matrix products: 27.5 us -> 12.4 us  [the longest x1 4.6 us: body(): total = lax.psum(jnp.dot(left, right.T, precision=HIGH), 'freq')]
    another operation x19 -> x14, other arithmetic: 100 us -> 108 us  [the longest x10 67.8 us: body(): factors = jnp.linalg.cholesky(jnp.stack([gram, node_gram]))]
  transfers between devices with their start and end apart: 5 -> 2, of which waited for: 5 -> 2; matrix products, arithmetic and copies ran while one was open for 1% -> 0% of each run, Pallas kernels for 0% -> 0%
where the time goes in v1:
time: 288 us
  waiting for transfers between devices  130 us (45%)
  other arithmetic  114 us (40%)
  matrix products  16.1 us (6%)
  between operations  14.3 us (5%)
  local copies, waits for them, and re-layouts  13.3 us (5%)
    psum x1, waiting for transfers between devices, body(): pivot_rows = lax.psum(picked, 'wave')  70.8 us
    another operation x10, other arithmetic, body(): factors = jnp.linalg.cholesky(jnp.stack([gram, node_gram]))  67.8 us
    psum x1, waiting for transfers between devices, body(): total = lax.psum(jnp.dot(left, right.T, precision=HIGH), 'freq')  59.4 us
    another operation x4, other arithmetic, body(): inverses = jax.scipy.linalg.solve_triangular(factors, eye, lower=True)  40.3 us
  transfers between devices with their start and end apart: 2, of which 2 were waited for; matrix products, arithmetic and copies ran while one was open for 0% of the time, Pallas kernels for 0%

profile of v1, /device:TPU:0, one launch (start us, length us, event | category | flops | bytes accessed | tf_op | source)
XLA Modules:
  0.0 288.0 jit_solution(7392579073697744297)
XLA Ops:
  7.2 0.0 all-reduce.4.cloned.1.call-start
  7.2 0.7 fusion.25
  7.9 0.7 compare_and_fusion
  8.6 4.0 %gather_fusion = f32[256,2048]{1,0:T(8,128)S(1)} fusion(f32[256,2048]{1,0:T(8,128)} %param.3, s32[1024]{0:T(1024)S(1)} %pad_clamp_fusion), kind=kCustom, calls=%fused_computation | custom fusion | bytes 4195328 | tf_op jit(solution)/shard_map/jit(_take)/gather | solution.py:17
  12.6 1.6 select_multiply_fusion
  14.2 0.0 all-reduce.4.cloned.1.call-update
  14.2 0.0 all-reduce.6.cloned.1.call-start
  14.3 0.5 copy-done.6
  14.9 0.9 convert_reduce_fusion
  15.8 0.0 copy-start
  15.8 70.8 %all-reduce.4.cloned.1.call-done = f32[256,2048]{1,0:T(8,128)} async-done(((f32[256,2048]{1,0:T(8,128)}), f32[256,2048]{1,0:T(8,128)}) %all-reduce.4.cloned.1.call-update) | async-done | bytes 2097168 | tf_op jit(solution)/shard_map/psum | solution.py:18
  86.6 2.0 broadcast_multiply_fusion
  88.5 0.0 copy-done
  88.6 0.2 copy-done.1
  88.8 4.6 %fusion = f32[512,512]{0,1:T(8,128)} fusion(f32[256,2048]{1,0:T(8,128)S(1)} %copy-done.1, f32[256,2048]{1,0:T(8,128)S(1)} %copy-done, f32[256,2048]{1,0:T(8,128)S(1)} %broadcast_multiply_fusion), kind=kOutput, calls=%fused_computation.6 | convolution fusion | flops 3223322624 | bytes 7340032 | tf_op jit(solution)/shard_map/dot_general | solution.py:24
  93.4 0.0 all-reduce.6.cloned.1.call-update
  93.5 59.4 %all-reduce.6.cloned.1.call-done = f32[512,512]{0,1:T(8,128)} async-done(((f32[512,512]{0,1:T(8,128)}), f32[512,512]{0,1:T(8,128)}) %all-reduce.6.cloned.1.call-update) | async-done | bytes 1048592 | tf_op jit(solution)/shard_map/psum | solution.py:24
  152.9 1.1 slice_bitcast_fusion.1
  153.9 0.8 pad_maximum_fusion.4
  154.8 1.2 copy.14
  156.0 0.1 fusion.3
  156.1 0.0 copy-start.4
  156.1 0.8 copy-done.4
  156.9 23.6 %custom-call.17 = f32[2,128,128]{2,1,0:T(8,128)S(1)} custom-call(f32[2,128,128]{2,1,0:T(8,128)S(1)} %cholesky.122), custom_call_target="Cholesky" | custom-call | tf_op jit(solution)/shard_map/jit(cholesky)/cholesky | solution.py:27
  180.6 19.7 %custom-call.18 = f32[2,1,128,128]{2,3,1,0:T(8,128)S(1)} custom-call(f32[2,1,128,128]{3,2,1,0:T(8,128)S(1)} %select_bitcast_fusion), custom_call_target="InvertDiagBlocksLowerTriangular" | custom-call | tf_op jit(solution)/shard_map/jit(cholesky)/cholesky | solution.py:27
  200.3 1.2 constant_dynamic-update-slice_fusion.1
  201.5 1.3 convolution_subtract_fusion.2
  202.8 23.5 %custom-call.19 = f32[2,128,128]{2,1,0:T(8,128)S(1)} custom-call(f32[2,128,128]{2,1,0:T(8,128)S(1)} %convolution_subtract_fusion.2), custom_call_target="Cholesky" | custom-call | tf_op jit(solution)/shard_map/jit(cholesky)/cholesky | solution.py:27
  226.3 0.2 compare_reduce_fusion
  226.4 0.1 select_select_fusion
  226.6 0.1 triangular_solve.66
  226.7 5.3 %while.1 = (s32[]{:T(128)}, f32[2,256,256]{2,1,0:T(8,128)S(1)}, s32[2,2]{1,0:T(2,128)S(1)}, f32[2,2,128,128]{3,2,0,1:T(8,128)}, s32[]{:T(128)}) while((s32[]{:T(128)}, f32[2,256,256]{2,1,0:T(8,128)S(1)}, s32[2,2]{1,0:T(2,128)S(1)}, f32[2,2,128,128]{3,2,0,1:T(8,128)}, s32[]{:T(128)}) %tuple.30), condition=%wide.while_cond, body=%wide.while_body.sunk | while | flops 2 | bytes 263277 | solution.py:29
  226.7 0.6 fusion.45
  227.3 2.0 bitcast_dynamic-update-slice_fusion.2
  229.3 0.6 fusion.45
  229.9 2.0 bitcast_dynamic-update-slice_fusion.2
  231.9 40.1 %custom-call.20 = f32[2,2,128,128]{2,3,1,0:T(8,128)S(1)} custom-call(f32[2,2,128,128]{3,2,1,0:T(8,128)} %bitcast.62), custom_call_target="InvertDiagBlocksLowerTriangular" | custom-call | tf_op jit(solution)/shard_map/jit(_solve_triangular)/vmap()/triangular_solve | solution.py:29
  272.1 0.4 fusion.14
  272.5 0.4 convolution_subtract_fusion.1
  272.9 0.4 fusion.13
  273.3 0.6 fusion.7
  273.9 0.4 fusion.19
  274.3 0.6 fusion.9
  274.9 0.0 copy-done.2
  274.9 1.2 fusion.22
  276.1 0.0 copy-start.3
  276.1 2.5 convolution_subtract_fusion
  278.7 2.5 fusion.33
  (23 shorter events, 0.3 us)
Async XLA Ops:
  7.2 79.4 %all-reduce.4.cloned.1.call-start = ((), (), s32[]{:S(2)}) async-start(), calls=%async_computation | async-start | bytes 4194304 | tf_op jit(solution)/shard_map/psum | solution.py:18
  14.2 0.7 copy-start.6
  14.2 138.6 %all-reduce.6.cloned.1.call-start = ((), (), s32[]{:S(2)}) async-start(), calls=%async_computation.1 | async-start | bytes 2097152 | tf_op jit(solution)/shard_map/psum | solution.py:24
  15.8 72.8 %copy-start = (f32[256,2048]{1,0:T(8,128)S(1)}, f32[256,2048]{1,0:T(8,128)}, u32[]{:S(2)}) copy-start(f32[256,2048]{1,0:T(8,128)} %param.3) | copy-start | bytes 6291460
  86.6 2.2 copy-start.1
  156.1 0.8 copy-start.4
  272.1 1.3 copy-start.5
  272.9 2.0 copy-start.2
  276.1 2.5 copy-start.3
Sparse Core Ops, SparseCore 0:
  14.3 72.1 all-reduce.3
  93.5 59.2 all-reduce.5

commit v2 on v1

v2 whole, which is shorter than its diff:
```python
import functools

import jax
import jax.numpy as jnp
from jax import lax
from jax.experimental import pallas as pl
from jax.experimental.pallas import tpu as pltpu
from jax.sharding import PartitionSpec as P

HIGH = lax.Precision.HIGH
FULL = lax.Precision.HIGHEST
MESH = pl.DeviceIdType.MESH
VMEM = pl.BlockSpec(memory_space=pltpu.VMEM)
SMEM = pl.BlockSpec(memory_space=pltpu.SMEM)


def dot(a, b):
    return lax.dot_general(
        a, b, (((1,), (0,)), ((), ())), precision=FULL, preferred_element_type=jnp.float32
    )


def dot_t(a, b):
    return lax.dot_general(
        a, b, (((1,), (1,)), ((), ())), precision=FULL, preferred_element_type=jnp.float32
    )


def factor_kernel(steps, size, total_ref, out_ref, work):
    count = steps * size
    subs = lax.broadcasted_iota(jnp.int32, (size, size), 0)
    lanes = lax.broadcasted_iota(jnp.int32, (size, size), 1)
    lane = lax.broadcasted_iota(jnp.int32, (1, size), 1)

    def block(m, i, j):
        return total_ref[i * size : (i + 1) * size, m * count + j * size : m * count + (j + 1) * size]

    mats = [[[block(m, i, j) for j in range(i + 1)] for i in range(steps)] for m in range(2)]
    lower = [{} for _ in range(2)]
    inverse = [{} for _ in range(2)]

    def eliminate(j, carry):
        for m in range(2):
            now = work[m]
            row = work[m, pl.ds(j, 1), :]
            here = lanes == j
            col = jnp.sum(jnp.where(here, now, 0.0), axis=1, keepdims=True)
            pivot = jnp.sum(jnp.where(lane == j, row, 0.0), axis=1, keepdims=True)
            row = jnp.where(lane == j, 1.0, row) / pivot
            below = subs > j
            work[m] = jnp.where(here & below, 0.0, now) - jnp.where(below, col, 0.0) * row
        return carry

    for b in range(steps):
        for m in range(2):
            work[m] = mats[m][b][b]
        lax.fori_loop(0, size, eliminate, 0)
        for m in range(2):
            done = work[m]
            diag = jnp.sum(jnp.where(subs == lanes, done, 0.0), axis=1, keepdims=True)
            unit = jnp.where(subs > lanes, done, jnp.where(subs == lanes, 1.0, 0.0))
            inverse[m][b, b] = unit / jnp.sqrt(diag)
            for i in range(b + 1, steps):
                lower[m][i, b] = dot_t(mats[m][i][b], inverse[m][b, b])
            for i in range(b + 1, steps):
                for j in range(b + 1, i + 1):
                    mats[m][i][j] = mats[m][i][j] - dot_t(lower[m][i, b], lower[m][j, b])
    for m in range(2):
        for j in range(steps):
            for i in range(j + 1, steps):
                acc = dot(lower[m][i, j], inverse[m][j, j])
                for k in range(j + 1, i):
                    acc = acc + dot(lower[m][i, k], inverse[m][k, j])
                inverse[m][i, j] = -dot(inverse[m][i, i], acc)
    zero = jnp.zeros((size, size), jnp.float32)
    full = [
        jnp.concatenate(
            [jnp.concatenate([inverse[m].get((i, j), zero) for j in range(steps)], axis=1) for i in range(steps)],
            axis=0,
        )
        for m in range(2)
    ]
    out_ref[:count, :] = full[0]
    rows = total_ref.shape[0] - count
    out_ref[count : count + rows, :] = dot(dot_t(total_ref[count:, :count], full[0]), full[0])
    out_ref[count + rows :, :] = dot(dot_t(total_ref[count:, count:], full[1]), full[1])


def factor(total, steps, size):
    count = steps * size
    rows = total.shape[0] - count
    return pl.pallas_call(
        functools.partial(factor_kernel, steps, size),
        out_shape=jax.ShapeDtypeStruct((count + 2 * rows, count), jnp.float32),
        in_specs=[VMEM],
        out_specs=VMEM,
        scratch_shapes=[pltpu.VMEM((2, size, size), jnp.float32)],
    )(total)


def freq_kernel(chips, part_ref, out_ref, half, near, far, send, recv):
    wave, freq = lax.axis_index("wave"), lax.axis_index("freq")
    core, chip = lax.rem(freq, 2), lax.div(freq, 2)
    rows = part_ref.shape[0]
    mid, piece = rows // 2, rows // 2 // chips
    mate = (wave, chip * 2 + 1 - core)
    others = [(wave, lax.rem(chip + d, chips) * 2 + core) for d in range(1, chips)]
    barrier = pltpu.get_barrier_semaphore()
    for peer in [mate] + others:
        pl.semaphore_signal(barrier, inc=1, device_id=peer, device_id_type=MESH)
    pl.semaphore_wait(barrier, chips)

    def copy(slot, src, dst, peer):
        return pltpu.make_async_remote_copy(
            src_ref=src, dst_ref=dst, send_sem=send.at[slot], recv_sem=recv.at[slot],
            device_id=peer, device_id_type=MESH,
        )

    def span(owner_core, owner_chip):
        return pl.ds(pl.multiple_of(owner_core * mid + owner_chip * piece, 8), piece)

    first = copy(0, part_ref.at[pl.ds(pl.multiple_of((1 - core) * mid, 8), mid)], near, mate)
    first.start()
    first.wait()
    half[...] = part_ref[pl.ds(pl.multiple_of(core * mid, 8), mid), :] + near[...]
    scatter = []
    for d in range(1, chips):
        to = lax.rem(chip + d, chips)
        scatter.append(
            copy(d, half.at[pl.ds(pl.multiple_of(to * piece, 8), piece)], far.at[d - 1], others[d - 1])
        )
        scatter[-1].start()
    for c in scatter:
        c.wait()
    total = half[pl.ds(pl.multiple_of(chip * piece, 8), piece), :]
    for d in range(1, chips):
        total = total + far[d - 1]
    out_ref[span(core, chip), :] = total
    own = out_ref.at[span(core, chip)]
    gather = [copy(chips + d - 1, own, own, others[d - 1]) for d in range(1, chips)]
    for c in gather:
        c.start()
    relay = [copy(2 * chips - 1, own, own, mate)]
    relay[0].start()
    for d in range(1, chips):
        gather[d - 1].wait_recv()
        came = out_ref.at[span(core, lax.rem(chip - d + chips, chips))]
        relay.append(copy(2 * chips - 1 + d, came, came, mate))
        relay[-1].start()
    for c in gather:
        c.wait_send()
    for c in relay:
        c.wait()


def freq_sum(part, freq, ident):
    chips = freq // 2
    rows, cols = part.shape
    slots = 3 * chips - 1
    return pl.pallas_call(
        functools.partial(freq_kernel, chips),
        out_shape=jax.ShapeDtypeStruct(part.shape, part.dtype),
        in_specs=[VMEM],
        out_specs=VMEM,
        scratch_shapes=[
            pltpu.VMEM((rows // 2, cols), jnp.float32),
            pltpu.VMEM((rows // 2, cols), jnp.float32),
            pltpu.VMEM((chips - 1, rows // 2 // chips, cols), jnp.float32),
            pltpu.SemaphoreType.DMA((slots,)),
            pltpu.SemaphoreType.DMA((slots,)),
        ],
        compiler_params=pltpu.CompilerParams(collective_id=ident, has_side_effects=True),
    )(part)


def wave_kernel(take_ref, slot_ref, rows_ref, out_ref, packed, gathered, send, recv, here):
    wave, freq = lax.axis_index("wave"), lax.axis_index("freq")
    y, x = lax.div(wave, 2), lax.rem(wave, 2)
    w_x, w_y = y * 2 + 1 - x, (1 - y) * 2 + x
    cap = packed.shape[0]
    mid = cap // 2
    barrier = pltpu.get_barrier_semaphore()
    for w in (w_x, w_y):
        pl.semaphore_signal(barrier, inc=1, device_id=(w, freq), device_id_type=MESH)

    def pack(k, carry):
        packed[pl.ds(k, 1), :] = rows_ref[pl.ds(take_ref[k], 1), :]
        return carry

    lax.fori_loop(0, cap, pack, 0, unroll=8)
    pl.semaphore_wait(barrier, 2)

    def place(owner, part):
        return gathered.at[pl.ds(pl.multiple_of(owner * cap + part * mid, 8), mid)]

    def copy(slot, src, dst, w):
        return pltpu.make_async_remote_copy(
            src_ref=src, dst_ref=dst, send_sem=send.at[slot], recv_sem=recv.at[slot],
            device_id=(w, freq), device_id_type=MESH,
        )

    def own(part):
        return packed.at[pl.ds(part * mid, mid)]

    x0, x1 = copy(0, own(0), place(wave, 0), w_x), copy(1, own(1), place(wave, 1), w_x)
    y1, y0 = copy(2, own(1), place(wave, 1), w_y), copy(3, own(0), place(wave, 0), w_y)
    for c in (x0, y1, x1, y0):
        c.start()
    stay = pltpu.make_async_copy(packed, gathered.at[pl.ds(pl.multiple_of(wave * cap, 8), cap)], here)
    stay.start()
    x0.wait_recv()
    fy = copy(4, place(w_x, 0), place(w_x, 0), w_y)
    fy.start()
    y1.wait_recv()
    fx = copy(5, place(w_y, 1), place(w_y, 1), w_x)
    fx.start()
    x1.wait_recv()
    y0.wait_recv()
    stay.wait()
    fy.wait_recv()
    fx.wait_recv()
    for c in (x0, x1, y0, y1, fx, fy):
        c.wait_send()

    def unpack(k, carry):
        out_ref[pl.ds(k, 1), :] = gathered[pl.ds(slot_ref[k], 1), :]
        return carry

    lax.fori_loop(0, out_ref.shape[0], unpack, 0, unroll=8)


def wave_rows(cap, ident, waves, wave, owner, rank, local_rows, waveforms):
    count = owner.shape[0]
    cols = waveforms.shape[1]
    order = jnp.arange(cap, dtype=jnp.int32)
    mine = (owner == wave)[None, :] & (rank[None, :] == order[:, None])
    take = jnp.sum(jnp.where(mine, local_rows[None, :], 0), axis=1)
    slot = owner * cap + rank
    return pl.pallas_call(
        wave_kernel,
        out_shape=jax.ShapeDtypeStruct((count, cols), jnp.float32),
        in_specs=[SMEM, SMEM, VMEM],
        out_specs=VMEM,
        scratch_shapes=[
            pltpu.VMEM((cap, cols), jnp.float32),
            pltpu.VMEM((waves * cap, cols), jnp.float32),
            pltpu.SemaphoreType.DMA((6,)),
            pltpu.SemaphoreType.DMA((6,)),
            pltpu.SemaphoreType.DMA,
        ],
        compiler_params=pltpu.CompilerParams(collective_id=ident, has_side_effects=True),
    )(take, slot, waveforms)


def gather_pivots(waveforms, picks, waves):
    rows_here = waveforms.shape[0]
    count = picks.shape[0]
    wave = lax.axis_index("wave")
    owner = lax.div(picks, rows_here)
    local_rows = lax.rem(picks, rows_here)
    if waves == 4:
        same = owner[:, None] == owner[None, :]
        order = jnp.arange(count, dtype=jnp.int32)
        rank = jnp.sum((same & (order[None, :] < order[:, None])).astype(jnp.int32), axis=1)
        cap = -(-(count * 11) // (waves * 8 * 16)) * 16
        fits = jnp.max(rank) < cap
        args = (waves, wave, owner, rank, local_rows, waveforms)
        return lax.cond(
            fits,
            lambda: wave_rows(cap, 0, *args),
            lambda: wave_rows(count, 1, *args),
        )
    picked = jnp.take(waveforms, local_rows, axis=0) * (owner == wave).astype(jnp.float32)[:, None]
    return lax.psum(picked, "wave")


def body(waves, freqs, waveforms, pivots, nodes):
    rows_here, cols_here = waveforms.shape
    steps, size = pivots.shape
    count = steps * size
    col_start = lax.axis_index("freq") * cols_here
    pivot_rows = gather_pivots(waveforms, pivots.reshape(-1), waves)
    columns = col_start + jnp.arange(cols_here, dtype=jnp.int32)
    node_count = jnp.sum((nodes[:, None] == columns[None, :]).astype(jnp.float32), axis=0)
    weighted = pivot_rows * node_count[None, :]
    left = jnp.concatenate([pivot_rows, waveforms], axis=0)
    right = jnp.concatenate([pivot_rows, weighted], axis=0)
    part = jnp.dot(left, right.T, precision=HIGH)
    if freqs == 8:
        total = freq_sum(part, freqs, 2)
    else:
        total = lax.psum(part, "freq")
    mixed = factor(total, steps, size)
    basis_rows = jnp.dot(mixed[:count], pivot_rows, precision=HIGH)
    residual = waveforms - jnp.dot(mixed[count : count + rows_here], pivot_rows, precision=HIGH)
    fitted = jnp.dot(mixed[count + rows_here :], pivot_rows, precision=HIGH)
    return (residual, basis_rows, fitted)


def solution(mesh):
    in_specs = (P("wave", "freq"), P(), P())
    out_specs = (P("wave", "freq"), P(None, "freq"), P("wave", "freq"))
    run = functools.partial(body, mesh.shape["wave"], mesh.shape["freq"])
    return jax.shard_map(run, mesh=mesh, in_specs=in_specs, out_specs=out_specs, check_vma=False)
```

time: 288 us -> 141 us (0.49)
  waiting for transfers between devices: 130 us -> 0 us
  Pallas kernels: 0 us -> 119 us
  other arithmetic: 114 us -> 4.53 us
  between operations: 14.3 us -> 1.34 us
  local copies, waits for them, and re-layouts: 13.3 us -> 1.36 us
  matrix products: 16.1 us -> 12.9 us
    psum x2 -> x0, waiting for transfers between devices: 130 us -> none  [the longest x1 70.8 us: body(): pivot_rows = lax.psum(picked, 'wave')]
    pallas_call x0 -> x3, Pallas kernels: none -> 119 us  [the longest x1 54.8 us: factor(): pl.pallas_call(functools.partial(factor_kernel, steps, size), out_shape=j...]
    another operation x14 -> x0, other arithmetic: 108 us -> none  [the longest x10 67.8 us: body(): factors = jnp.linalg.cholesky(jnp.stack([gram, node_gram]))]
    another operation x12 -> x0, local copies, waits for them, and re-layouts: 7.68 us -> none
    gather x1 -> x0, local copies, waits for them, and re-layouts: 3.99 us -> none  [body(): jnp.take(waveforms, jnp.clip(local_rows, 0, rows_here - 1), axis=0)]
    another operation x5 -> x0, matrix products: 3.69 us -> none  [the longest x2 2.48 us: body(): factors = jnp.linalg.cholesky(jnp.stack([gram, node_gram]))]
    dot_general x7 -> x4, matrix products: 12.4 us -> 12.9 us  [the longest x1 4.54 us: body(): part = jnp.dot(left, right.T, precision=HIGH)]
  transfers between devices with their start and end apart: 2 -> 0, of which waited for: 2 -> 0; matrix products, arithmetic and copies ran while one was open for 0% -> 0% of each run, Pallas kernels for 0% -> 0%
where the time goes in v2:
time: 141 us; the launch traced here: 139 us
  Pallas kernels  119 us (84%)
  matrix products  12.9 us (9%)
  other arithmetic  4.53 us (3%)
    pallas_call x1, Pallas kernels, factor(): pl.pallas_call(functools.partial(factor_kernel, steps, size), out_shape=j...  54.8 us
    pallas_call x1, Pallas kernels, wave_rows(): pl.pallas_call(wave_kernel, out_shape=jax.ShapeDtypeStruct((count, cols),...  33.1 us
    pallas_call x1, Pallas kernels, freq_sum(): pl.pallas_call(functools.partial(freq_kernel, chips), out_shape=jax.Shape...  31.1 us
    dot_general x1, matrix products, body(): part = jnp.dot(left, right.T, precision=HIGH)  4.54 us
    dot_general x1, matrix products, body(): fitted = jnp.dot(mixed[count + rows_here:], pivot_rows, precision=HIGH)  3.45 us

profile of v2, /device:TPU:0, one launch (start us, length us, event | category | flops | bytes accessed | tf_op | source)
XLA Modules:
  0.0 139.2 jit_solution(11281254823375189475)
XLA Ops:
  0.6 0.7 negate_select_fusion
  1.3 0.2 convert_reduce_fusion.1
  1.5 0.6 reduce_max.9
  2.8 1.6 %convert_reduce_fusion = f32[2048]{0:T(1024)S(1)} fusion(s32[2048]{0:T(1024)S(1)} %iota_add_fusion, s32[1024]{0:T(1024)} %param.7), kind=kLoop, calls=%fused_computation.10 | loop fusion | flops 6289408 | bytes 20480 | tf_op jit(solution)/shard_map/reduce_sum | solution.py:284
  4.4 34.4 %conditional.1 = (f32[256,2048]{1,0:T(8,128)S(1)}) conditional(s32[]{:T(128)} %convert_element_type.10, (s32[]{:T(128)}, s32[256]{0:T(256)S(1)}, s32[256]{0:T(256)S(1)}, s32[256]{0:T(256)S(1)}, f32[256,2048]{1,0:T(8,128)}) %tuple.14, (s32[]{:T(128)}, s32[256]{0:T(256)S(1)}, s32[256]{0:T(256)S(1)}, s32[256]{0:T(256)S(1)}, f32[256,2048]{1,0:T(8,128)}) %tuple.14), branch_computations={%region_2.4_spmd, %region_4.6_spmd} | conditional | flops 262656 | bytes 7692 | solution.py:268
  4.4 0.6 select_reduce_fusion.1.take_ref
  5.1 0.6 multiply_add_fusion.1.slot_ref
  5.6 33.1 %branch_1_fun.1 = f32[256,2048]{1,0:T(8,128)S(1)} custom-call(s32[96]{0:T(128)} %select_reduce_fusion.1.take_ref, s32[256]{0:T(256)} %multiply_add_fusion.1.slot_ref, f32[256,2048]{1,0:T(8,128)} %get-tuple-element.32.rows_ref), custom_call_target="tpu_custom_call" | custom-call | tf_op jit(solution)/shard_map/cond/branch_1_fun/pallas_call | solution.py:239
  38.8 0.0 copy-start
  38.8 0.2 broadcast_multiply_fusion
  39.0 1.3 copy-done
  40.4 4.5 %fusion.2.part_ref = f32[512,512]{1,0:T(8,128)} fusion(f32[256,2048]{1,0:T(8,128)S(1)} %get-tuple-element.38, f32[256,2048]{1,0:T(8,128)S(1)} %copy-done, f32[256,2048]{1,0:T(8,128)S(1)} %broadcast_multiply_fusion), kind=kOutput, calls=%fused_computation.13 | convolution fusion | flops 3223322624 | bytes 7340032 | tf_op jit(solution)/shard_map/dot_general | solution.py:288
  44.9 31.1 %shard_map.58.total_ref = f32[512,512]{1,0:T(8,128)} custom-call(f32[512,512]{1,0:T(8,128)} %fusion.2.part_ref), custom_call_target="tpu_custom_call" | custom-call | tf_op jit(solution)/shard_map/pallas_call | solution.py:160
  76.0 54.8 %shard_map.59 = f32[768,256]{1,0:T(8,128)} custom-call(f32[512,512]{1,0:T(8,128)} %shard_map.58.total_ref), custom_call_target="tpu_custom_call" | custom-call | tf_op jit(solution)/shard_map/pallas_call | solution.py:92
  130.9 0.0 copy-start.2
  130.9 3.4 %fusion.5 = f32[256,2048]{1,0:T(8,128)} fusion(f32[256,2048]{1,0:T(8,128)S(1)} %get-tuple-element.38, f32[768,256]{1,0:T(8,128)} %shard_map.59), kind=kOutput, calls=%fused_computation.18 | convolution fusion | flops 805306368 | bytes 4456448 | tf_op jit(solution)/shard_map/dot_general | solution.py:296
  134.3 0.0 copy-done.2
  134.3 0.0 copy-start.1
  134.3 2.4 %fusion.7 = f32[256,2048]{1,0:T(8,128)} fusion(f32[256,2048]{1,0:T(8,128)S(1)} %get-tuple-element.38, f32[768,256]{1,0:T(8,128)S(1)} %copy-done.2), kind=kOutput, calls=%fused_computation.20 | convolution fusion | flops 805306368 | bytes 4456448 | tf_op jit(solution)/shard_map/dot_general | solution.py:294
  136.7 0.0 copy-done.1
  136.7 2.5 %convolution_subtract_fusion = f32[256,2048]{1,0:T(8,128)} fusion(f32[256,2048]{1,0:T(8,128)S(1)} %copy-done.1, f32[256,2048]{1,0:T(8,128)S(1)} %get-tuple-element.38, f32[768,256]{1,0:T(8,128)S(1)} %copy-done.2), kind=kOutput, calls=%fused_computation.16 | convolution fusion | flops 805830656 | bytes 6553600 | tf_op jit(solution)/shard_map/dot_general | solution.py:295
  (2 shorter events, 0.0 us)
Async XLA Ops:
  38.8 1.6 %copy-start = (f32[256,2048]{1,0:T(8,128)S(1)}, f32[256,2048]{1,0:T(8,128)}, u32[]{:S(2)}) copy-start(f32[256,2048]{1,0:T(8,128)} %param.5) | copy-start | bytes 6291460
  130.9 3.5 %copy-start.2 = (f32[768,256]{1,0:T(8,128)S(1)}, f32[768,256]{1,0:T(8,128)}, u32[]{:S(2)}) copy-start(f32[768,256]{1,0:T(8,128)} %shard_map.59) | copy-start | bytes 2359300
  134.3 2.4 %copy-start.1 = (f32[256,2048]{1,0:T(8,128)S(1)}, f32[256,2048]{1,0:T(8,128)}, u32[]{:S(2)}) copy-start(f32[256,2048]{1,0:T(8,128)} %param.5) | copy-start | bytes 6291460

commit v3 on v2

--- a/solution.py
+++ b/solution.py
@@ -26,60 +26,62 @@
     )
 
 
+def factorize(blk, count, total_ref, out_ref, work):
+    blocks = count // blk
+    subs = lax.broadcasted_iota(jnp.int32, (blk, 2 * blk), 0)
+    lanes = lax.broadcasted_iota(jnp.int32, (blk, 2 * blk), 1)
+    inner = lax.rem(lanes, blk)
+    base = lanes - inner
+
+    cols = [
+        [total_ref[c * blk : count, m * count + c * blk : m * count + (c + 1) * blk] for c in range(blocks)]
+        for m in range(2)
+    ]
+    acc = [jnp.zeros((count, count), jnp.float32) for _ in range(2)]
+    parts = [[], []]
+
+    def eliminate(j, carry):
+        now = work[...]
+        row = work[pl.ds(j, 1), :]
+        col = jnp.take_along_axis(now, base + j, axis=1)
+        pivot = jnp.take_along_axis(jnp.broadcast_to(row, (8, 2 * blk)), base[:8] + j, axis=1)[:1]
+        at = inner == j
+        row = jnp.where(at[:1], 1.0, row) / pivot
+        below = subs > j
+        work[...] = jnp.where(at & below, 0.0, now) - jnp.where(below, col, 0.0) * row
+        return carry
+
+    for b in range(blocks):
+        work[...] = jnp.concatenate([cols[0][b][:blk], cols[1][b][:blk]], axis=1)
+        lax.fori_loop(0, blk, eliminate, 0, unroll=4)
+        done = work[...]
+        for m in range(2):
+            mine = done[:, m * blk : (m + 1) * blk]
+            sub = lax.broadcasted_iota(jnp.int32, (blk, blk), 0)
+            lane = lax.broadcasted_iota(jnp.int32, (blk, blk), 1)
+            diag = jnp.sum(jnp.where(sub == lane, mine, 0.0), axis=1, keepdims=True)
+            unit = jnp.where(sub > lane, mine, jnp.where(sub == lane, 1.0, 0.0))
+            small = unit / jnp.sqrt(diag)
+            pads = [jnp.zeros((blk, b * blk), jnp.float32)] if b > 0 else []
+            pads.append(small)
+            if b + 1 < blocks:
+                pads.append(jnp.zeros((blk, count - (b + 1) * blk), jnp.float32))
+            wide = jnp.concatenate(pads, axis=1)
+            if b > 0:
+                wide = wide - dot(small, acc[m][:blk])
+            parts[m].append(wide)
+            if b + 1 < blocks:
+                panel = dot_t(cols[m][b][blk:], small)
+                for c in range(b + 1, blocks):
+                    low = (c - b - 1) * blk
+                    cols[m][c] = cols[m][c] - dot_t(panel[low:], panel[low : low + blk])
+                acc[m] = acc[m][blk:] + dot(panel, wide)
+    return [jnp.concatenate(p, axis=0) for p in parts]
+
+
 def factor_kernel(steps, size, total_ref, out_ref, work):
     count = steps * size
-    subs = lax.broadcasted_iota(jnp.int32, (size, size), 0)
-    lanes = lax.broadcasted_iota(jnp.int32, (size, size), 1)
-    lane = lax.broadcasted_iota(jnp.int32, (1, size), 1)
-
-    def block(m, i, j):
-        return total_ref[i * size : (i + 1) * size, m * count + j * size : m * count + (j + 1) * size]
-
-    mats = [[[block(m, i, j) for j in range(i + 1)] for i in range(steps)] for m in range(2)]
-    lower = [{} for _ in range(2)]
-    inverse = [{} for _ in range(2)]
-
-    def eliminate(j, carry):
-        for m in range(2):
-            now = work[m]
-            row = work[m, pl.ds(j, 1), :]
-            here = lanes == j
-            col = jnp.sum(jnp.where(here, now, 0.0), axis=1, keepdims=True)
-            pivot = jnp.sum(jnp.where(lane == j, row, 0.0), axis=1, keepdims=True)
-            row = jnp.where(lane == j, 1.0, row) / pivot
-            below = subs > j
-            work[m] = jnp.where(here & below, 0.0, now) - jnp.where(below, col, 0.0) * row
-        return carry
-
-    for b in range(steps):
-        for m in range(2):
-            work[m] = mats[m][b][b]
-        lax.fori_loop(0, size, eliminate, 0)
-        for m in range(2):
-            done = work[m]
-            diag = jnp.sum(jnp.where(subs == lanes, done, 0.0), axis=1, keepdims=True)
-            unit = jnp.where(subs > lanes, done, jnp.where(subs == lanes, 1.0, 0.0))
-            inverse[m][b, b] = unit / jnp.sqrt(diag)
-            for i in range(b + 1, steps):
-                lower[m][i, b] = dot_t(mats[m][i][b], inverse[m][b, b])
-            for i in range(b + 1, steps):
-                for j in range(b + 1, i + 1):
-                    mats[m][i][j] = mats[m][i][j] - dot_t(lower[m][i, b], lower[m][j, b])
-    for m in range(2):
-        for j in range(steps):
-            for i in range(j + 1, steps):
-                acc = dot(lower[m][i, j], inverse[m][j, j])
-                for k in range(j + 1, i):
-                    acc = acc + dot(lower[m][i, k], inverse[m][k, j])
-                inverse[m][i, j] = -dot(inverse[m][i, i], acc)
-    zero = jnp.zeros((size, size), jnp.float32)
-    full = [
-        jnp.concatenate(
-            [jnp.concatenate([inverse[m].get((i, j), zero) for j in range(steps)], axis=1) for i in range(steps)],
-            axis=0,
-        )
-        for m in range(2)
-    ]
+    full = factorize(work.shape[0], count, total_ref, out_ref, work)
     out_ref[:count, :] = full[0]
     rows = total_ref.shape[0] - count
     out_ref[count : count + rows, :] = dot(dot_t(total_ref[count:, :count], full[0]), full[0])
@@ -94,7 +96,7 @@
         out_shape=jax.ShapeDtypeStruct((count + 2 * rows, count), jnp.float32),
         in_specs=[VMEM],
         out_specs=VMEM,
-        scratch_shapes=[pltpu.VMEM((2, size, size), jnp.float32)],
+        scratch_shapes=[pltpu.VMEM((size // 2, size), jnp.float32)],
     )(total)
 
 

time: 141 us -> 115 us (0.82)
  Pallas kernels: 119 us -> 93.5 us
    pallas_call x1, Pallas kernels: 54.8 us -> 29.2 us  [factor(): pl.pallas_call(functools.partial(factor_kernel, steps, size), out_shape=j...]
where the time goes in v3:
time: 115 us; the launch traced here: 114 us
  Pallas kernels  93.5 us (81%)
  matrix products  12.9 us (11%)
  other arithmetic  4.53 us (4%)
  local copies, waits for them, and re-layouts  1.36 us (1%)
  between operations  1.34 us (1%)
    pallas_call x1, Pallas kernels, wave_rows(): pl.pallas_call(wave_kernel, out_shape=jax.ShapeDtypeStruct((count, cols),...  33.1 us
    pallas_call x1, Pallas kernels, freq_sum(): pl.pallas_call(functools.partial(freq_kernel, chips), out_shape=jax.Shape...  31.1 us
    pallas_call x1, Pallas kernels, factor(): pl.pallas_call(functools.partial(factor_kernel, steps, size), out_shape=j...  29.2 us
    dot_general x1, matrix products, body(): part = jnp.dot(left, right.T, precision=HIGH)  4.54 us
    dot_general x1, matrix products, body(): fitted = jnp.dot(mixed[count + rows_here:], pivot_rows, precision=HIGH)  3.44 us
    dot_general x1, matrix products, body(): jnp.dot(mixed[count:count + rows_here], pivot_rows, precision=HIGH)  2.5 us
    dot_general x1, matrix products, body(): basis_rows = jnp.dot(mixed[:count], pivot_rows, precision=HIGH)  2.42 us

profile of v3, /device:TPU:0, one launch (start us, length us, event | category | flops | bytes accessed | tf_op | source)
XLA Modules:
  0.0 113.6 jit_solution(2909075786101785782)
XLA Ops:
  0.6 0.7 negate_select_fusion
  1.3 0.2 convert_reduce_fusion.1
  1.5 0.6 reduce_max.9
  2.8 1.6 %convert_reduce_fusion = f32[2048]{0:T(1024)S(1)} fusion(s32[2048]{0:T(1024)S(1)} %iota_add_fusion, s32[1024]{0:T(1024)} %param.7), kind=kLoop, calls=%fused_computation.10 | loop fusion | flops 6289408 | bytes 20480 | tf_op jit(solution)/shard_map/reduce_sum | solution.py:286
  4.4 34.4 %conditional.1 = (f32[256,2048]{1,0:T(8,128)S(1)}) conditional(s32[]{:T(128)} %convert_element_type.10, (s32[]{:T(128)}, s32[256]{0:T(256)S(1)}, s32[256]{0:T(256)S(1)}, s32[256]{0:T(256)S(1)}, f32[256,2048]{1,0:T(8,128)}) %tuple.14, (s32[]{:T(128)}, s32[256]{0:T(256)S(1)}, s32[256]{0:T(256)S(1)}, s32[256]{0:T(256)S(1)}, f32[256,2048]{1,0:T(8,128)}) %tuple.14), branch_computations={%region_2.4_spmd, %region_4.6_spmd} | conditional | flops 262656 | bytes 7692 | solution.py:270
  4.4 0.6 select_reduce_fusion.1.take_ref
  5.1 0.6 multiply_add_fusion.1.slot_ref
  5.6 33.1 %branch_1_fun.1 = f32[256,2048]{1,0:T(8,128)S(1)} custom-call(s32[96]{0:T(128)} %select_reduce_fusion.1.take_ref, s32[256]{0:T(256)} %multiply_add_fusion.1.slot_ref, f32[256,2048]{1,0:T(8,128)} %get-tuple-element.32.rows_ref), custom_call_target="tpu_custom_call" | custom-call | tf_op jit(solution)/shard_map/cond/branch_1_fun/pallas_call | solution.py:241
  38.8 0.0 copy-start
  38.8 0.2 broadcast_multiply_fusion
  39.0 1.3 %copy-done = f32[256,2048]{1,0:T(8,128)S(1)} copy-done((f32[256,2048]{1,0:T(8,128)S(1)}, f32[256,2048]{1,0:T(8,128)}, u32[]{:S(2)}) %copy-start) | copy-done | bytes 2097176
  40.4 4.5 %fusion.2.part_ref = f32[512,512]{1,0:T(8,128)} fusion(f32[256,2048]{1,0:T(8,128)S(1)} %get-tuple-element.38, f32[256,2048]{1,0:T(8,128)S(1)} %copy-done, f32[256,2048]{1,0:T(8,128)S(1)} %broadcast_multiply_fusion), kind=kOutput, calls=%fused_computation.13 | convolution fusion | flops 3223322624 | bytes 7340032 | tf_op jit(solution)/shard_map/dot_general | solution.py:290
  44.9 31.1 %shard_map.58.total_ref = f32[512,512]{1,0:T(8,128)} custom-call(f32[512,512]{1,0:T(8,128)} %fusion.2.part_ref), custom_call_target="tpu_custom_call" | custom-call | tf_op jit(solution)/shard_map/pallas_call | solution.py:162
  76.0 29.2 %shard_map.59 = f32[768,256]{1,0:T(8,128)} custom-call(f32[512,512]{1,0:T(8,128)} %shard_map.58.total_ref), custom_call_target="tpu_custom_call" | custom-call | tf_op jit(solution)/shard_map/pallas_call | solution.py:94
  105.3 0.0 copy-start.2
  105.3 3.4 %fusion.5 = f32[256,2048]{1,0:T(8,128)} fusion(f32[256,2048]{1,0:T(8,128)S(1)} %get-tuple-element.38, f32[768,256]{1,0:T(8,128)} %shard_map.59), kind=kOutput, calls=%fused_computation.18 | convolution fusion | flops 805306368 | bytes 4456448 | tf_op jit(solution)/shard_map/dot_general | solution.py:298
  108.7 0.0 copy-done.2
  108.7 0.0 copy-start.1
  108.7 2.4 %fusion.7 = f32[256,2048]{1,0:T(8,128)} fusion(f32[256,2048]{1,0:T(8,128)S(1)} %get-tuple-element.38, f32[768,256]{1,0:T(8,128)S(1)} %copy-done.2), kind=kOutput, calls=%fused_computation.20 | convolution fusion | flops 805306368 | bytes 4456448 | tf_op jit(solution)/shard_map/dot_general | solution.py:296
  111.1 0.0 copy-done.1
  111.1 2.5 %convolution_subtract_fusion = f32[256,2048]{1,0:T(8,128)} fusion(f32[256,2048]{1,0:T(8,128)S(1)} %copy-done.1, f32[256,2048]{1,0:T(8,128)S(1)} %get-tuple-element.38, f32[768,256]{1,0:T(8,128)S(1)} %copy-done.2), kind=kOutput, calls=%fused_computation.16 | convolution fusion | flops 805830656 | bytes 6553600 | tf_op jit(solution)/shard_map/dot_general | solution.py:297
  (2 shorter events, 0.0 us)
Async XLA Ops:
  38.8 1.6 %copy-start = (f32[256,2048]{1,0:T(8,128)S(1)}, f32[256,2048]{1,0:T(8,128)}, u32[]{:S(2)}) copy-start(f32[256,2048]{1,0:T(8,128)} %param.5) | copy-start | bytes 6291460
  105.3 3.4 %copy-start.2 = (f32[768,256]{1,0:T(8,128)S(1)}, f32[768,256]{1,0:T(8,128)}, u32[]{:S(2)}) copy-start(f32[768,256]{1,0:T(8,128)} %shard_map.59) | copy-start | bytes 2359300
  108.7 2.4 %copy-start.1 = (f32[256,2048]{1,0:T(8,128)S(1)}, f32[256,2048]{1,0:T(8,128)}, u32[]{:S(2)}) copy-start(f32[256,2048]{1,0:T(8,128)} %param.5) | copy-start | bytes 6291460

commit v4 on v3

--- a/solution.py
+++ b/solution.py
@@ -26,7 +26,7 @@
     )
 
 
-def factorize(blk, count, total_ref, out_ref, work):
+def factorize(blk, count, fetch, work, between):
     blocks = count // blk
     subs = lax.broadcasted_iota(jnp.int32, (blk, 2 * blk), 0)
     lanes = lax.broadcasted_iota(jnp.int32, (blk, 2 * blk), 1)
@@ -34,8 +34,7 @@
     base = lanes - inner
 
     cols = [
-        [total_ref[c * blk : count, m * count + c * blk : m * count + (c + 1) * blk] for c in range(blocks)]
-        for m in range(2)
+        [fetch(m, c) for c in range(blocks)] for m in range(2)
     ]
     acc = [jnp.zeros((count, count), jnp.float32) for _ in range(2)]
     parts = [[], []]
@@ -76,98 +75,185 @@
                     low = (c - b - 1) * blk
                     cols[m][c] = cols[m][c] - dot_t(panel[low:], panel[low : low + blk])
                 acc[m] = acc[m][blk:] + dot(panel, wide)
+        between(b)
     return [jnp.concatenate(p, axis=0) for p in parts]
 
 
-def factor_kernel(steps, size, total_ref, out_ref, work):
-    count = steps * size
-    full = factorize(work.shape[0], count, total_ref, out_ref, work)
+def solve(full, cross, rows, count, out_ref):
     out_ref[:count, :] = full[0]
-    rows = total_ref.shape[0] - count
-    out_ref[count : count + rows, :] = dot(dot_t(total_ref[count:, :count], full[0]), full[0])
-    out_ref[count + rows :, :] = dot(dot_t(total_ref[count:, count:], full[1]), full[1])
-
-
-def factor(total, steps, size):
-    count = steps * size
+    out_ref[count : count + rows, :] = dot(dot_t(cross[:, :count], full[0]), full[0])
+    out_ref[count + rows :, :] = dot(dot_t(cross[:, count:], full[1]), full[1])
+
+
+def factor_kernel(count, total_ref, out_ref, work):
+    blk = work.shape[0]
+
+    def fetch(m, c):
+        return total_ref[c * blk : count, m * count + c * blk : m * count + (c + 1) * blk]
+
+    full = factorize(blk, count, fetch, work, lambda b: None)
+    solve(full, total_ref[count:, :], total_ref.shape[0] - count, count, out_ref)
+
+
+def factor(total, count):
     rows = total.shape[0] - count
     return pl.pallas_call(
-        functools.partial(factor_kernel, steps, size),
+        functools.partial(factor_kernel, count),
         out_shape=jax.ShapeDtypeStruct((count + 2 * rows, count), jnp.float32),
         in_specs=[VMEM],
         out_specs=VMEM,
-        scratch_shapes=[pltpu.VMEM((size // 2, size), jnp.float32)],
+        scratch_shapes=[pltpu.VMEM((64, 128), jnp.float32)],
     )(total)
 
 
-def freq_kernel(chips, part_ref, out_ref, half, near, far, send, recv):
+def sum_factor_kernel(
+    chips, count, part_ref, out_ref, near_g, half_g, far_g, gram, near_x, half_x, far_x, cross, work, send, recv
+):
     wave, freq = lax.axis_index("wave"), lax.axis_index("freq")
     core, chip = lax.rem(freq, 2), lax.div(freq, 2)
-    rows = part_ref.shape[0]
-    mid, piece = rows // 2, rows // 2 // chips
+    size = count // 2
+    tall = 3 * size
+    step_g = tall // chips
+    rows = part_ref.shape[0] - count
+    mid = rows // 2
+    step_x = mid // chips
     mate = (wave, chip * 2 + 1 - core)
     others = [(wave, lax.rem(chip + d, chips) * 2 + core) for d in range(1, chips)]
     barrier = pltpu.get_barrier_semaphore()
     for peer in [mate] + others:
         pl.semaphore_signal(barrier, inc=1, device_id=peer, device_id_type=MESH)
     pl.semaphore_wait(barrier, chips)
-
-    def copy(slot, src, dst, peer):
+    used = [0]
+
+    def copy(src, dst, peer):
+        slot = used[0]
+        used[0] += 1
         return pltpu.make_async_remote_copy(
             src_ref=src, dst_ref=dst, send_sem=send.at[slot], recv_sem=recv.at[slot],
             device_id=peer, device_id_type=MESH,
         )
 
-    def span(owner_core, owner_chip):
-        return pl.ds(pl.multiple_of(owner_core * mid + owner_chip * piece, 8), piece)
-
-    first = copy(0, part_ref.at[pl.ds(pl.multiple_of((1 - core) * mid, 8), mid)], near, mate)
-    first.start()
-    first.wait()
-    half[...] = part_ref[pl.ds(pl.multiple_of(core * mid, 8), mid), :] + near[...]
-    scatter = []
-    for d in range(1, chips):
-        to = lax.rem(chip + d, chips)
-        scatter.append(
-            copy(d, half.at[pl.ds(pl.multiple_of(to * piece, 8), piece)], far.at[d - 1], others[d - 1])
-        )
-        scatter[-1].start()
-    for c in scatter:
-        c.wait()
-    total = half[pl.ds(pl.multiple_of(chip * piece, 8), piece), :]
-    for d in range(1, chips):
-        total = total + far[d - 1]
-    out_ref[span(core, chip), :] = total
-    own = out_ref.at[span(core, chip)]
-    gather = [copy(chips + d - 1, own, own, others[d - 1]) for d in range(1, chips)]
-    for c in gather:
-        c.start()
-    relay = [copy(2 * chips - 1, own, own, mate)]
-    relay[0].start()
-    for d in range(1, chips):
-        gather[d - 1].wait_recv()
-        came = out_ref.at[span(core, lax.rem(chip - d + chips, chips))]
-        relay.append(copy(2 * chips - 1 + d, came, came, mate))
-        relay[-1].start()
-    for c in gather:
+    def at(start, length):
+        return pl.ds(pl.multiple_of(start, 8), length)
+
+    def block(i, owner):
+        row, col = ((0, 0), (1, 0), (1, 1))[i]
+        return pl.ds(row * size, size), pl.ds(pl.multiple_of(owner * count + col * size, 128), size)
+
+    swaps = [copy(part_ref.at[block(i, 1 - core)], near_g.at[pl.ds(i * size, size)], mate) for i in range(3)]
+    swap_x = copy(part_ref.at[at(count + (1 - core) * mid, mid)], near_x, mate)
+    for c in swaps:
+        c.start()
+    swap_x.start()
+
+    def all_to_all(half, far, step):
+        return [
+            copy(half.at[at(lax.rem(chip + d, chips) * step, step)], far.at[d - 1], others[d - 1])
+            for d in range(1, chips)
+        ]
+
+    def gathered(whole, tall, step):
+        own = whole.at[at(core * tall + chip * step, step)]
+        return [copy(own, own, others[d - 1]) for d in range(1, chips)], copy(own, own, mate)
+
+    def relays(whole, tall, step):
+        out = []
+        for d in range(1, chips):
+            came = whole.at[at(core * tall + lax.rem(chip - d + chips, chips) * step, step)]
+            out.append(copy(came, came, mate))
+        return out
+
+    def reduce(half, far, step):
+        total = half[at(chip * step, step), :]
+        for d in range(1, chips):
+            total = total + far[d - 1]
+        return total
+
+    for i in range(3):
+        swaps[i].wait_recv()
+        here = pl.ds(i * size, size)
+        half_g[here, :] = part_ref[block(i, core)] + near_g[here, :]
+    scatter_g = all_to_all(half_g, far_g, step_g)
+    for c in scatter_g:
+        c.start()
+    swap_x.wait_recv()
+    half_x[...] = part_ref[at(count + core * mid, mid), :] + near_x[...]
+    for c in scatter_g:
+        c.wait_recv()
+    gram[at(core * tall + chip * step_g, step_g), :] = reduce(half_g, far_g, step_g)
+    sends_g, mate_g = gathered(gram, tall, step_g)
+    for c in sends_g:
+        c.start()
+    mate_g.start()
+    scatter_x = all_to_all(half_x, far_x, step_x)
+    for c in scatter_x:
+        c.start()
+    relay_g = relays(gram, tall, step_g)
+    for d in range(chips - 1):
+        sends_g[d].wait_recv()
+        relay_g[d].start()
+    mate_g.wait_recv()
+    for c in relay_g:
+        c.wait_recv()
+    sends_x, mate_x = gathered(cross, mid, step_x)
+    relay_x = relays(cross, mid, step_x)
+    blk = work.shape[0]
+
+    def fetch(m, c):
+        top = m * tall
+        low = c * blk
+        if low < size:
+            return gram[top + low : top + 2 * size, low : low + blk]
+        return gram[top + size + low : top + tall, low - size : low - size + blk]
+
+    def between(b):
+        if b == 1:
+            for c in scatter_x:
+                c.wait_recv()
+            cross[at(core * mid + chip * step_x, step_x), :] = reduce(half_x, far_x, step_x)
+            for c in sends_x:
+                c.start()
+            mate_x.start()
+        if b == 3:
+            for d in range(chips - 1):
+                sends_x[d].wait_recv()
+                relay_x[d].start()
+
+    full = factorize(blk, count, fetch, work, between)
+    mate_x.wait_recv()
+    for c in relay_x:
+        c.wait_recv()
+    solve(full, cross[...], rows, count, out_ref)
+    for c in swaps + [swap_x, mate_g, mate_x] + scatter_g + scatter_x + sends_g + sends_x + relay_g + relay_x:
         c.wait_send()
-    for c in relay:
-        c.wait()
-
-
-def freq_sum(part, freq, ident):
+
+
+def sum_factor(part, count, freq, ident):
     chips = freq // 2
-    rows, cols = part.shape
-    slots = 3 * chips - 1
+    rows = part.shape[0] - count
+    size = count // 2
+    tall = 3 * size
+    cols = part.shape[1]
+    slots = 4 + 6 * (chips - 1) + 2
+
+    def buffer(*shape):
+        return pltpu.VMEM(shape, jnp.float32)
+
     return pl.pallas_call(
-        functools.partial(freq_kernel, chips),
-        out_shape=jax.ShapeDtypeStruct(part.shape, part.dtype),
+        functools.partial(sum_factor_kernel, chips, count),
+        out_shape=jax.ShapeDtypeStruct((count + 2 * rows, count), jnp.float32),
         in_specs=[VMEM],
         out_specs=VMEM,
         scratch_shapes=[
-            pltpu.VMEM((rows // 2, cols), jnp.float32),
-            pltpu.VMEM((rows // 2, cols), jnp.float32),
-            pltpu.VMEM((chips - 1, rows // 2 // chips, cols), jnp.float32),
+            buffer(tall, size),
+            buffer(tall, size),
+            buffer(chips - 1, tall // chips, size),
+            buffer(2 * tall, size),
+            buffer(rows // 2, cols),
+            buffer(rows // 2, cols),
+            buffer(chips - 1, rows // 2 // chips, cols),
+            buffer(rows, cols),
+            buffer(64, 128),
             pltpu.SemaphoreType.DMA((slots,)),
             pltpu.SemaphoreType.DMA((slots,)),
         ],
@@ -189,7 +275,7 @@
         packed[pl.ds(k, 1), :] = rows_ref[pl.ds(take_ref[k], 1), :]
         return carry
 
-    lax.fori_loop(0, cap, pack, 0, unroll=8)
+    lax.fori_loop(0, mid, pack, 0, unroll=8)
     pl.semaphore_wait(barrier, 2)
 
     def place(owner, part):
@@ -206,7 +292,9 @@
 
     x0, x1 = copy(0, own(0), place(wave, 0), w_x), copy(1, own(1), place(wave, 1), w_x)
     y1, y0 = copy(2, own(1), place(wave, 1), w_y), copy(3, own(0), place(wave, 0), w_y)
-    for c in (x0, y1, x1, y0):
+    x0.start()
+    lax.fori_loop(mid, cap, pack, 0, unroll=8)
+    for c in (y1, x1, y0):
         c.start()
     stay = pltpu.make_async_copy(packed, gathered.at[pl.ds(pl.multiple_of(wave * cap, 8), cap)], here)
     stay.start()
@@ -264,14 +352,11 @@
         same = owner[:, None] == owner[None, :]
         order = jnp.arange(count, dtype=jnp.int32)
         rank = jnp.sum((same & (order[None, :] < order[:, None])).astype(jnp.int32), axis=1)
-        cap = -(-(count * 11) // (waves * 8 * 16)) * 16
-        fits = jnp.max(rank) < cap
+        caps = [-(-count * 5 // (waves * 64)) * 16, -(-count * 3 // (waves * 32)) * 16, count]
+        most = jnp.max(rank) + 1
         args = (waves, wave, owner, rank, local_rows, waveforms)
-        return lax.cond(
-            fits,
-            lambda: wave_rows(cap, 0, *args),
-            lambda: wave_rows(count, 1, *args),
-        )
+        tier = jnp.sum((most > jnp.array(caps[:-1])).astype(jnp.int32))
+        return lax.switch(tier, [functools.partial(wave_rows, cap, i, *args) for i, cap in enumerate(caps)])
     picked = jnp.take(waveforms, local_rows, axis=0) * (owner == wave).astype(jnp.float32)[:, None]
     return lax.psum(picked, "wave")
 
@@ -288,11 +373,10 @@
     left = jnp.concatenate([pivot_rows, waveforms], axis=0)
     right = jnp.concatenate([pivot_rows, weighted], axis=0)
     part = jnp.dot(left, right.T, precision=HIGH)
-    if freqs == 8:
-        total = freq_sum(part, freqs, 2)
+    if freqs == 8 and count == 256:
+        mixed = sum_factor(part, count, freqs, 3)
     else:
-        total = lax.psum(part, "freq")
-    mixed = factor(total, steps, size)
+        mixed = factor(lax.psum(part, "freq"), count)
     basis_rows = jnp.dot(mixed[:count], pivot_rows, precision=HIGH)
     residual = waveforms - jnp.dot(mixed[count : count + rows_here], pivot_rows, precision=HIGH)
     fitted = jnp.dot(mixed[count + rows_here :], pivot_rows, precision=HIGH)

time: 115 us -> 98.1 us (0.85)
  Pallas kernels: 93.5 us -> 75.7 us
  other arithmetic: 4.53 us -> 5.82 us
    pallas_call x2 -> x1, Pallas kernels: 60.3 us -> 46.6 us  [sum_factor(): pl.pallas_call(functools.partial(sum_factor_kernel, chips, count), out_sh...]
    pallas_call x1, Pallas kernels: 33.1 us -> 29.1 us  [wave_rows(): pl.pallas_call(wave_kernel, out_shape=jax.ShapeDtypeStruct((count, cols),...]
    reduce_sum x0 -> x1, other arithmetic: none -> 1.3 us  [gather_pivots(): tier = jnp.sum((most > jnp.array(caps[:-1])).astype(jnp.int32))]
where the time goes in v4:
time: 98.1 us; the launch traced here: 97.8 us
  Pallas kernels  75.7 us (77%)
  matrix products  12.9 us (13%)
  other arithmetic  5.82 us (6%)
  between operations  2 us (2%)
  local copies, waits for them, and re-layouts  1.36 us (1%)
    pallas_call x1, Pallas kernels, sum_factor(): pl.pallas_call(functools.partial(sum_factor_kernel, chips, count), out_sh...  46.6 us
    pallas_call x1, Pallas kernels, wave_rows(): pl.pallas_call(wave_kernel, out_shape=jax.ShapeDtypeStruct((count, cols),...  29.1 us
    dot_general x1, matrix products, body(): part = jnp.dot(left, right.T, precision=HIGH)  4.54 us
    dot_general x1, matrix products, body(): fitted = jnp.dot(mixed[count + rows_here:], pivot_rows, precision=HIGH)  3.44 us
    dot_general x1, matrix products, body(): jnp.dot(mixed[count:count + rows_here], pivot_rows, precision=HIGH)  2.5 us
    dot_general x1, matrix products, body(): basis_rows = jnp.dot(mixed[:count], pivot_rows, precision=HIGH)  2.42 us

profile of v4, /device:TPU:0, one launch (start us, length us, event | category | flops | bytes accessed | tf_op | source)
XLA Modules:
  0.0 97.8 jit_solution(3585618860225609574)
XLA Ops:
  0.6 0.7 negate_select_fusion
  1.3 0.2 convert_reduce_fusion.1
  1.5 0.6 reduce_max.9
  2.8 1.3 %fusion.12 = s32[]{:T(128)} fusion(s32[2]{0:T(128)} %constant.41.clone, s32[]{:T(128)S(6)} %add.22), kind=kLoop, calls=%fused_computation.37 | loop fusion | flops 5 | bytes 16 | tf_op jit(solution)/shard_map/reduce_sum | solution.py:358
  4.8 1.6 %convert_reduce_fusion = f32[2048]{0:T(1024)S(1)} fusion(s32[2048]{0:T(1024)S(1)} %iota_add_fusion, s32[1024]{0:T(1024)} %param.9), kind=kLoop, calls=%fused_computation.15 | loop fusion | flops 6289408 | bytes 20480 | tf_op jit(solution)/shard_map/reduce_sum | solution.py:371
  6.3 30.3 %conditional.1 = (f32[256,2048]{1,0:T(8,128)S(1)}) conditional(s32[]{:T(128)} %clamp.3, (s32[]{:T(128)}, s32[256]{0:T(256)S(1)}, s32[256]{0:T(256)S(1)}, s32[256]{0:T(256)S(1)}, f32[256,2048]{1,0:T(8,128)}) %tuple.17, (s32[]{:T(128)}, s32[256]{0:T(256)S(1)}, s32[256]{0:T(256)S(1)}, s32[256]{0:T(256)S(1)}, ...), branch_computations={%region_3.5_spmd, %region_5.7_spmd, %region_7.9_spmd} | conditional | flops 262656 | bytes 7692 | solution.py:359
  6.4 0.6 select_reduce_fusion.take_ref
  7.0 0.6 multiply_add_fusion.slot_ref
  7.6 29.1 %branch_0_fun.1 = f32[256,2048]{1,0:T(8,128)S(1)} custom-call(s32[80]{0:T(128)} %select_reduce_fusion.take_ref, s32[256]{0:T(256)} %multiply_add_fusion.slot_ref, f32[256,2048]{1,0:T(8,128)} %get-tuple-element.38.rows_ref), custom_call_target="tpu_custom_call" | custom-call | tf_op jit(solution)/shard_map/cond/branch_0_fun/pallas_call | solution.py:329
  36.7 0.0 copy-start
  36.7 0.2 broadcast_multiply_fusion
  36.9 1.3 %copy-done = f32[256,2048]{1,0:T(8,128)S(1)} copy-done((f32[256,2048]{1,0:T(8,128)S(1)}, f32[256,2048]{1,0:T(8,128)}, u32[]{:S(2)}) %copy-start) | copy-done | bytes 2097176
  38.3 4.5 %fusion.3.part_ref = f32[512,512]{1,0:T(8,128)} fusion(f32[256,2048]{1,0:T(8,128)S(1)} %get-tuple-element.54, f32[256,2048]{1,0:T(8,128)S(1)} %copy-done, f32[256,2048]{1,0:T(8,128)S(1)} %broadcast_multiply_fusion), kind=kOutput, calls=%fused_computation.18 | convolution fusion | flops 3223322624 | bytes 7340032 | tf_op jit(solution)/shard_map/dot_general | solution.py:375
  42.8 46.6 %shard_map.67 = f32[768,256]{1,0:T(8,128)} custom-call(f32[512,512]{1,0:T(8,128)} %fusion.3.part_ref), custom_call_target="tpu_custom_call" | custom-call | tf_op jit(solution)/shard_map/pallas_call | solution.py:242
  89.4 0.0 copy-start.2
  89.4 3.4 %fusion.6 = f32[256,2048]{1,0:T(8,128)} fusion(f32[256,2048]{1,0:T(8,128)S(1)} %get-tuple-element.54, f32[768,256]{1,0:T(8,128)} %shard_map.67), kind=kOutput, calls=%fused_computation.23 | convolution fusion | flops 805306368 | bytes 4456448 | tf_op jit(solution)/shard_map/dot_general | solution.py:382
  92.9 0.0 copy-done.2
  92.9 0.0 copy-start.1
  92.9 2.4 %fusion.8 = f32[256,2048]{1,0:T(8,128)} fusion(f32[256,2048]{1,0:T(8,128)S(1)} %get-tuple-element.54, f32[768,256]{1,0:T(8,128)S(1)} %copy-done.2), kind=kOutput, calls=%fused_computation.25 | convolution fusion | flops 805306368 | bytes 4456448 | tf_op jit(solution)/shard_map/dot_general | solution.py:380
  95.3 0.0 copy-done.1
  95.3 2.5 %convolution_subtract_fusion = f32[256,2048]{1,0:T(8,128)} fusion(f32[256,2048]{1,0:T(8,128)S(1)} %copy-done.1, f32[256,2048]{1,0:T(8,128)S(1)} %get-tuple-element.54, f32[768,256]{1,0:T(8,128)S(1)} %copy-done.2), kind=kOutput, calls=%fused_computation.21 | convolution fusion | flops 805830656 | bytes 6553600 | tf_op jit(solution)/shard_map/dot_general | solution.py:381
  (2 shorter events, 0.0 us)
Async XLA Ops:
  36.7 1.6 %copy-start = (f32[256,2048]{1,0:T(8,128)S(1)}, f32[256,2048]{1,0:T(8,128)}, u32[]{:S(2)}) copy-start(f32[256,2048]{1,0:T(8,128)} %param.7) | copy-start | bytes 6291460
  89.4 3.5 %copy-start.2 = (f32[768,256]{1,0:T(8,128)S(1)}, f32[768,256]{1,0:T(8,128)}, u32[]{:S(2)}) copy-start(f32[768,256]{1,0:T(8,128)} %shard_map.67) | copy-start | bytes 2359300
  92.9 2.4 %copy-start.1 = (f32[256,2048]{1,0:T(8,128)S(1)}, f32[256,2048]{1,0:T(8,128)}, u32[]{:S(2)}) copy-start(f32[256,2048]{1,0:T(8,128)} %param.7) | copy-start | bytes 6291460
